TPU v7x, 32 devices: a whole 2x2x4 slice. The times are simulated.
32 devices in a mesh: tok: 8 (over y, x, core), blk: 4 (over z).
Axes of the slice: x: 2, y: 2, z: 4, core: 2. Of those that a mesh axis runs over, the one named last changes fastest.
Arguments:
- activations: bfloat16 [4096, 4096], P('tok', 'blk'), may hold values from -52 to 52, as said below
- out_grads: bfloat16 [4096, 4096], P('tok', 'blk'), may hold values from -52 to 52, as said below
Outputs:
- act_inverse: float32 [4096, 4096], P(('tok', 'blk'))
- grad_inverse: float32 [4096, 4096], P(('tok', 'blk'))
Inputs may be any that keep to these rules, and one draw needn't show every extreme that they name: `activations`: real entries. `out_grads`: real entries.
All inputs are finite; a program needn't handle non-finite values.
Results may differ from a plain program's by a relative error of at most 0.02.
Values may be sent and summed in bfloat16 or wider, within the bound.
A program may use at most 64 MiB of HBM per device.

v0:
```python
import jax
import jax.numpy as jnp
from jax import lax
from jax.sharding import PartitionSpec as P

D = 4096


damping = 0.3
epsilon = 1e-06
divisor = 2.0


def column_squares(data):
    values = data.astype(jnp.float32)
    return jnp.sum(values * values, axis=0)


def fold_product(row_block, tile):
    return jnp.dot(
        row_block,
        lax.all_gather(tile, "tok", axis=0, tiled=True),
        preferred_element_type=jnp.float32,
    )


def newton_steps(scaled, identity):
    half = scaled.astype(jnp.bfloat16)
    row_block = lax.all_gather(half, "blk", axis=1, tiled=True)
    square = fold_product(row_block, half)
    cube = fold_product(row_block, square.astype(jnp.bfloat16))
    return 4.0 * identity - 6.0 * scaled + 4.0 * square - cube


def body(activations, out_grads):
    tok_count = lax.axis_size("tok")
    blk_count = lax.axis_size("blk")
    tok_id = lax.axis_index("tok")
    blk_id = lax.axis_index("blk")
    token_count = activations.shape[0] * tok_count
    tile_rows = D // tok_count
    tile_cols = D // blk_count
    full_acts, full_grads = (
        lax.all_gather(activations, "blk", axis=1, tiled=True),
        lax.all_gather(out_grads, "blk", axis=1, tiled=True),
    )
    sums_act, sums_grad = (
        lax.psum(column_squares(full_acts).astype(jnp.bfloat16), "tok").astype(jnp.float32),
        lax.psum(column_squares(full_grads).astype(jnp.bfloat16), "tok").astype(jnp.float32),
    )
    row_ids = tok_id * tile_rows + jnp.arange(tile_rows, dtype=jnp.int32)
    col_ids = blk_id * tile_cols + jnp.arange(tile_cols, dtype=jnp.int32)
    identity = (row_ids[:, None] == col_ids[None, :]).astype(jnp.float32)

    def damped_tile(full, local, sums):
        gram_tile = lax.psum_scatter(
            lax.dot_general(
                full, local, (((0,), (0,)), ((), ())), preferred_element_type=jnp.float32
            ).astype(jnp.bfloat16),
            "tok",
            scatter_dimension=0,
            tiled=True,
        ).astype(jnp.float32)
        inverse = lax.rsqrt(sums / token_count + epsilon)
        inverse_rows = lax.dynamic_slice_in_dim(inverse, tok_id * tile_rows, tile_rows)
        inverse_cols = lax.dynamic_slice_in_dim(inverse, blk_id * tile_cols, tile_cols)
        return (
            gram_tile / token_count * inverse_rows[:, None] * inverse_cols[None, :]
            + damping * identity
        )

    damped_act = damped_tile(full_acts, activations, sums_act)
    damped_grad = damped_tile(full_grads, out_grads, sums_grad)
    results = []
    for damped in (damped_act, damped_grad):
        scaled = damped / divisor
        result_tile = newton_steps(scaled, identity)
        results.append(
            lax.all_to_all(
                result_tile.astype(jnp.bfloat16), "blk", split_axis=0, concat_axis=1, tiled=True
            ).astype(result_tile.dtype)
        )
    return (results[0], results[1])


def solution(mesh):
    placed = (P("tok", "blk"), P("tok", "blk"))
    return jax.shard_map(
        body,
        mesh=mesh,
        in_specs=placed,
        out_specs=(P(("tok", "blk"), None), P(("tok", "blk"), None)),
        check_vma=False,
    )
```

profile of v0, /device:TPU:0, one launch (start us, length us, event | category | flops | bytes accessed | tf_op | source)
XLA Modules:
  0.0 763.5 jit_solution(1316433522095304969)
XLA Ops:
  7.2 0.0 copy-start.1
  7.2 0.0 all-gather.9.cloned.1.call-start
  7.2 0.7 all-gather.9.cloned.1.call-update
  7.9 0.0 all-gather.17.cloned.1.call-start
  8.0 0.7 all-gather.17.cloned.1.call-update
  8.7 0.0 reduce-scatter.3.cloned.1.call-start
  8.7 84.3 %all-gather.9.cloned.1.call-done = bf16[512,4096]{1,0:T(8,128)(2,1)} async-done(((bf16[512,1024]{1,0:T(8,128)(2,1)}), bf16[512,4096]{1,0:T(8,128)(2,1)}) %all-gather.9.cloned.1.call-update) | async-done | bytes 4194320 | tf_op jit(solution)/shard_map/all_gather | solution.py:44
  93.0 0.0 copy-done.1
  93.0 9.1 %convolution_convert_fusion.1 = bf16[4096,1024]{1,0:T(8,128)(2,1)} fusion(bf16[512,4096]{1,0:T(8,128)(2,1)} %all-gather.9.cloned.1.call-done, bf16[512,1024]{1,0:T(8,128)(2,1)S(1)} %copy-done.1), kind=kOutput, calls=%fused_computation.3 | convolution fusion | flops 4299161600 | bytes 13631488 | tf_op jit(solution)/shard_map/dot_general | solution.py:57
  102.1 0.0 copy-start.2
  102.1 0.0 reduce-scatter.3.cloned.1.call-update
  102.2 0.0 reduce-scatter.5.cloned.1.call-start
  102.2 71.7 %all-gather.17.cloned.1.call-done = bf16[512,4096]{1,0:T(8,128)(2,1)} async-done(((bf16[512,1024]{1,0:T(8,128)(2,1)}), bf16[512,4096]{1,0:T(8,128)(2,1)}) %all-gather.17.cloned.1.call-update) | async-done | bytes 4194320 | tf_op jit(solution)/shard_map/all_gather | solution.py:45
  173.9 0.0 copy-done.2
  173.9 9.0 %convolution_convert_fusion = bf16[4096,1024]{1,0:T(8,128)(2,1)} fusion(bf16[512,4096]{1,0:T(8,128)(2,1)} %all-gather.17.cloned.1.call-done, bf16[512,1024]{1,0:T(8,128)(2,1)S(1)} %copy-done.2), kind=kOutput, calls=%fused_computation.2 | convolution fusion | flops 4299161600 | bytes 13631488 | tf_op jit(solution)/shard_map/dot_general | solution.py:57
  182.9 0.0 reduce-scatter.5.cloned.1.call-update
  182.9 0.0 all-gather.19.cloned.1.call-start
  183.0 0.0 copy-start
  183.0 4.2 multiply_reduce_fusion
  187.1 1.0 copy-done
  188.2 0.9 multiply_reduce_fusion.1
  189.1 24.5 %all-reduce = (bf16[4096]{0:T(1024)(128)(2,1)S(1)}, bf16[4096]{0:T(1024)(128)(2,1)S(1)}) all-reduce(bf16[4096]{0:T(1024)(128)(2,1)S(1)} %multiply_reduce_fusion.1, bf16[4096]{0:T(1024)(128)(2,1)S(1)} %multiply_reduce_fusion), channel_id=1, replica_groups=mesh['tok'=8,'blk'=4] {'tok'}, use_global_device_ids=true, to_apply=%region_2.0 | all-reduce | flops 8192 | bytes 32768 | tf_op jit(solution)/shard_map/psum | solution.py:48
  213.6 0.1 dynamic-slice_multiply_fusion
  213.7 0.1 dynamic-slice_multiply_fusion.1
  213.8 33.8 %reduce-scatter.3.cloned.1.call-done = bf16[512,1024]{1,0:T(8,128)(2,1)} async-done(((bf16[4096,1024]{1,0:T(8,128)(2,1)}), bf16[512,1024]{1,0:T(8,128)(2,1)}) %reduce-scatter.3.cloned.1.call-update) | async-done | bytes 1048592 | tf_op jit(solution)/shard_map/reduce_scatter | solution.py:56
  247.6 74.8 %reduce-scatter.5.cloned.1.call-done = bf16[512,1024]{1,0:T(8,128)(2,1)} async-done(((bf16[4096,1024]{1,0:T(8,128)(2,1)}), bf16[512,1024]{1,0:T(8,128)(2,1)}) %reduce-scatter.5.cloned.1.call-update) | async-done | bytes 1048592 | tf_op jit(solution)/shard_map/reduce_scatter | solution.py:56
  322.4 3.8 multiply_convert_fusion
  326.2 0.0 all-gather.19.cloned.1.call-update
  326.2 0.0 all-gather.21.cloned.1.call-start
  326.3 0.5 all-gather.21.cloned.1.call-update
  326.8 0.0 all-gather.11.cloned.1.call-start
  326.9 0.7 all-gather.11.cloned.1.call-update
  327.6 0.0 all-gather.13.cloned.1.call-start
  327.6 0.7 all-gather.13.cloned.1.call-update
  328.3 0.0 all-gather.23.cloned.1.call-start
  328.4 78.8 %all-gather.19.cloned.1.call-done = bf16[512,4096]{1,0:T(8,128)(2,1)} async-done(((bf16[512,1024]{1,0:T(8,128)(2,1)}), bf16[512,4096]{1,0:T(8,128)(2,1)}) %all-gather.19.cloned.1.call-update) | async-done | bytes 4194320 | tf_op jit(solution)/shard_map/all_gather | solution.py:29
  407.1 55.1 %all-gather.21.cloned.1.call-done = bf16[4096,1024]{1,0:T(8,128)(2,1)} async-done(((bf16[512,1024]{1,0:T(8,128)(2,1)}), bf16[4096,1024]{1,0:T(8,128)(2,1)}) %all-gather.21.cloned.1.call-update) | async-done | bytes 8388624 | tf_op jit(solution)/shard_map/all_gather | solution.py:22
  462.2 10.1 %fusion.9 = (bf16[512,1024]{1,0:T(8,128)(2,1)}, f32[512,1024]{1,0:T(8,128)S(1)}) fusion(bf16[512,4096]{1,0:T(8,128)(2,1)} %all-gather.19.cloned.1.call-done, bf16[4096,1024]{1,0:T(8,128)(2,1)} %all-gather.21.cloned.1.call-done), kind=kOutput, calls=%fused_computation.26 | convolution fusion | flops 4295491584 | bytes 15728640 | tf_op jit(solution)/shard_map/dot_general | solution.py:20
  472.4 0.0 all-gather.23.cloned.1.call-update
  472.4 0.0 copy-start.4
  472.4 0.2 all-gather.15.cloned.1.call-start
  472.6 72.5 %all-gather.11.cloned.1.call-done = bf16[512,4096]{1,0:T(8,128)(2,1)} async-done(((bf16[512,1024]{1,0:T(8,128)(2,1)}), bf16[512,4096]{1,0:T(8,128)(2,1)}) %all-gather.11.cloned.1.call-update) | async-done | bytes 4194320 | tf_op jit(solution)/shard_map/all_gather | solution.py:29
  545.1 55.2 %all-gather.13.cloned.1.call-done = bf16[4096,1024]{1,0:T(8,128)(2,1)} async-done(((bf16[512,1024]{1,0:T(8,128)(2,1)}), bf16[4096,1024]{1,0:T(8,128)(2,1)}) %all-gather.13.cloned.1.call-update) | async-done | bytes 8388624 | tf_op jit(solution)/shard_map/all_gather | solution.py:22
  600.4 10.8 %fusion.8 = (bf16[512,1024]{1,0:T(8,128)(2,1)}, f32[512,1024]{1,0:T(8,128)}) fusion(bf16[512,4096]{1,0:T(8,128)(2,1)} %all-gather.11.cloned.1.call-done, bf16[4096,1024]{1,0:T(8,128)(2,1)} %all-gather.13.cloned.1.call-done), kind=kOutput, calls=%fused_computation.25 | convolution fusion | flops 4295491584 | bytes 15728640 | tf_op jit(solution)/shard_map/dot_general | solution.py:20
  611.2 0.0 all-gather.15.cloned.1.call-update
  611.2 45.4 %all-gather.23.cloned.1.call-done = bf16[4096,1024]{1,0:T(8,128)(2,1)} async-done(((bf16[512,1024]{1,0:T(8,128)(2,1)}), bf16[4096,1024]{1,0:T(8,128)(2,1)}) %all-gather.23.cloned.1.call-update) | async-done | bytes 8388624 | tf_op jit(solution)/shard_map/all_gather | solution.py:22
  656.6 0.0 copy-done.4
  656.6 10.6 %fusion.7 = bf16[512,1024]{1,0:T(8,128)(2,1)} fusion(f32[512,1024]{1,0:T(8,128)S(1)} %get-tuple-element.9, bf16[512,1024]{1,0:T(8,128)(2,1)S(1)} %copy-done.4, bf16[512,4096]{1,0:T(8,128)(2,1)} %all-gather.19.cloned.1.call-done, bf16[4096,1024]{1,0:T(8,128)(2,1)} %all-gather.23.cloned.1.call-done, f32[1024]{0:T(1024)S(1)} %dynamic_slice.15, ...), kind=kOutput, calls=%fused_computation.14 | convolution fusion | flops 4301783040 | bytes 16789504 | tf_op jit(solution)/shard_map/dot_general | solution.py:20
  667.2 0.0 copy-start.3
  667.2 4.7 all-to-all-start.1
  671.9 41.2 %all-gather.15.cloned.1.call-done = bf16[4096,1024]{1,0:T(8,128)(2,1)} async-done(((bf16[512,1024]{1,0:T(8,128)(2,1)}), bf16[4096,1024]{1,0:T(8,128)(2,1)}) %all-gather.15.cloned.1.call-update) | async-done | bytes 8388624 | tf_op jit(solution)/shard_map/all_gather | solution.py:22
  713.2 0.0 copy-done.3
  713.2 11.1 %fusion.4 = bf16[512,1024]{1,0:T(8,128)(2,1)} fusion(f32[512,1024]{1,0:T(8,128)} %get-tuple-element.7, bf16[512,1024]{1,0:T(8,128)(2,1)S(1)} %copy-done.3, bf16[512,4096]{1,0:T(8,128)(2,1)} %all-gather.11.cloned.1.call-done, bf16[4096,1024]{1,0:T(8,128)(2,1)} %all-gather.15.cloned.1.call-done, f32[1024]{0:T(1024)S(1)} %dynamic_slice.13, ...), kind=kOutput, calls=%fused_computation.11 | convolution fusion | flops 4301783040 | bytes 16789504 | tf_op jit(solution)/shard_map/dot_general | solution.py:20
  724.3 0.0 all-to-all-done.1
  724.3 4.6 all-to-all-start
  728.9 0.2 convert_bitcast_fusion
  729.1 1.5 copy.7
  730.6 24.4 %all-to-all-done = bf16[4,128,1024]{2,1,0:T(8,128)(2,1)S(1)} async-done(((bf16[4,128,1024]{2,1,0:T(8,128)(2,1)}), bf16[4,128,1024]{2,1,0:T(8,128)(2,1)S(1)}, u32[]{:S(2)}, u32[]{:S(2)}) %all-to-all-start) | async-done | bytes 1048608 | tf_op jit(solution)/shard_map/all_to_all | solution.py:79
  755.0 0.2 convert_bitcast_fusion.1
  755.2 1.5 copy.6
  (5 shorter events, 0.0 us)
Async XLA Ops:
  7.2 85.9 %copy-start.1 = (bf16[512,1024]{1,0:T(8,128)(2,1)S(1)}, bf16[512,1024]{1,0:T(8,128)(2,1)}, u32[]{:S(2)}) copy-start(bf16[512,1024]{1,0:T(8,128)(2,1)} %param.2) | copy-start | bytes 3145732
  7.2 85.9 %all-gather.9.cloned.1.call-start = ((), (), s32[]{:S(2)}) async-start(), calls=%async_computation.4 | async-start | bytes 5242880 | tf_op jit(solution)/shard_map/all_gather | solution.py:44
  7.9 166.0 %all-gather.17.cloned.1.call-start = ((), (), s32[]{:S(2)}) async-start(), calls=%async_computation.9 | async-start | bytes 5242880 | tf_op jit(solution)/shard_map/all_gather | solution.py:45
  8.7 238.9 %reduce-scatter.3.cloned.1.call-start = ((), (), s32[]{:S(2)}) async-start(), calls=%async_computation.5 | async-start | bytes 9437184 | tf_op jit(solution)/shard_map/reduce_scatter | solution.py:56
  102.1 71.7 %copy-start.2 = (bf16[512,1024]{1,0:T(8,128)(2,1)S(1)}, bf16[512,1024]{1,0:T(8,128)(2,1)}, u32[]{:S(2)}) copy-start(bf16[512,1024]{1,0:T(8,128)(2,1)} %param.3) | copy-start | bytes 3145732
  102.2 220.2 %reduce-scatter.5.cloned.1.call-start = ((), (), s32[]{:S(2)}) async-start(), calls=%async_computation.10 | async-start | bytes 9437184 | tf_op jit(solution)/shard_map/reduce_scatter | solution.py:56
  182.9 224.3 %all-gather.19.cloned.1.call-start = ((), (), s32[]{:S(2)}) async-start(), calls=%async_computation.11 | async-start | bytes 5242880 | tf_op jit(solution)/shard_map/all_gather | solution.py:29
  183.0 5.2 copy-start
  326.2 136.0 %all-gather.21.cloned.1.call-start = ((), (), s32[]{:S(2)}) async-start(), calls=%async_computation.12 | async-start | bytes 9437184 | tf_op jit(solution)/shard_map/all_gather | solution.py:22
  326.8 218.3 %all-gather.11.cloned.1.call-start = ((), (), s32[]{:S(2)}) async-start(), calls=%async_computation.6 | async-start | bytes 5242880 | tf_op jit(solution)/shard_map/all_gather | solution.py:29
  327.6 272.8 %all-gather.13.cloned.1.call-start = ((), (), s32[]{:S(2)}) async-start(), calls=%async_computation.7 | async-start | bytes 9437184 | tf_op jit(solution)/shard_map/all_gather | solution.py:22
  328.3 328.3 %all-gather.23.cloned.1.call-start = ((), (), s32[]{:S(2)}) async-start(), calls=%async_computation.13 | async-start | bytes 9437184 | tf_op jit(solution)/shard_map/all_gather | solution.py:22
  472.4 184.2 %copy-start.4 = (bf16[512,1024]{1,0:T(8,128)(2,1)S(1)}, bf16[512,1024]{1,0:T(8,128)(2,1)}, u32[]{:S(2)}) copy-start(bf16[512,1024]{1,0:T(8,128)(2,1)} %reduce-scatter.5.cloned.1.call-done) | copy-start | bytes 3145732
  472.4 240.8 %all-gather.15.cloned.1.call-start = ((), (), s32[]{:S(2)}) async-start(), calls=%async_computation.8 | async-start | bytes 9437184 | tf_op jit(solution)/shard_map/all_gather | solution.py:22
  667.2 46.0 %copy-start.3 = (bf16[512,1024]{1,0:T(8,128)(2,1)S(1)}, bf16[512,1024]{1,0:T(8,128)(2,1)}, u32[]{:S(2)}) copy-start(bf16[512,1024]{1,0:T(8,128)(2,1)} %reduce-scatter.3.cloned.1.call-done) | copy-start | bytes 3145732
  667.2 57.0 %all-to-all-start.1 = ((bf16[4,128,1024]{2,1,0:T(8,128)(2,1)}), bf16[4,128,1024]{2,1,0:T(8,128)(2,1)S(1)}, u32[]{:S(2)}, u32[]{:S(2)}) async-start(bf16[4,128,1024]{2,1,0:T(8,128)(2,1)} %bitcast.2), calls=%async_computation.3 | async-start | bytes 2097152 | tf_op jit(solution)/shard_map/all_to_all | solution.py:79
  724.3 30.7 %all-to-all-start = ((bf16[4,128,1024]{2,1,0:T(8,128)(2,1)}), bf16[4,128,1024]{2,1,0:T(8,128)(2,1)S(1)}, u32[]{:S(2)}, u32[]{:S(2)}) async-start(bf16[4,128,1024]{2,1,0:T(8,128)(2,1)} %bitcast), calls=%async_computation.1 | async-start | bytes 2097152 | tf_op jit(solution)/shard_map/all_to_all | solution.py:79
Sparse Core Ops, SparseCore 0:
  9.6 83.4 all-gather.8
  94.6 79.2 all-gather.16
  177.3 70.1 reduce-scatter.2
  250.9 71.4 reduce-scatter.4
  326.4 80.7 all-gather.18
  409.5 52.7 all-gather.20
  464.4 80.7 all-gather.10
  547.6 52.7 all-gather.12
  602.3 54.2 all-gather.22
  658.9 54.2 all-gather.14
where the time goes:
time: 764 us
  waiting for transfers between devices  641 us (84%)
  matrix products  60.7 us (8%)
  blocking collectives  24.5 us (3%)
  between operations  14.3 us (2%)
  starting transfers between devices  9.9 us (1%)
  other arithmetic  9.53 us (1%)
    all_gather x4, waiting for transfers between devices, fold_product(): lax.all_gather(tile, 'tok', axis=0, tiled=True)  197 us
    all_gather x2, waiting for transfers between devices, newton_steps(): row_block = lax.all_gather(half, 'blk', axis=1, tiled=True)  151 us
    reduce_scatter x2, waiting for transfers between devices, damped_tile(): lax.psum_scatter(lax.dot_general(full, local, (((0,), (0,)), ((), ())), p...  109 us
    all_gather x1, waiting for transfers between devices, body(): lax.all_gather(activations, 'blk', axis=1, tiled=True)  84.3 us
    all_gather x1, waiting for transfers between devices, body(): lax.all_gather(out_grads, 'blk', axis=1, tiled=True)  71.7 us
    dot_general x4, matrix products, fold_product(): jnp.dot(row_block, lax.all_gather(tile, 'tok', axis=0, tiled=True), prefe...  42.6 us
    psum x1, blocking collectives, body(): lax.psum(column_squares(full_acts).astype(jnp.bfloat16), 'tok')  24.5 us
    all_to_all x2, waiting for transfers between devices, body(): lax.all_to_all(result_tile.astype(jnp.bfloat16), 'blk', split_axis=0, con...  24.4 us
  transfers between devices with their start and end apart: 12, of which 11 were waited for; matrix products, arithmetic and copies ran while one was open for 9% of the time, Pallas kernels for 0%

commit v1 on v0

v1 whole, which is shorter than its diff:
```python
import functools

import jax
import jax.numpy as jnp
from jax import lax
from jax.experimental import pallas as pl
from jax.experimental.pallas import tpu as pltpu
from jax.sharding import PartitionSpec as P

damping = 0.3
epsilon = 1e-06
divisor = 2.0
gathered_budget = 32 * 1024 * 1024
MESH = pl.DeviceIdType.MESH


def column_squares(data):
    values = data.astype(jnp.float32)
    return jnp.sum(values * values, axis=0)


def fold_product(row_block, tile):
    return jnp.dot(
        row_block,
        lax.all_gather(tile, "tok", axis=0, tiled=True),
        preferred_element_type=jnp.float32,
    )


def newton_steps(scaled, identity):
    half = scaled.astype(jnp.bfloat16)
    row_block = lax.all_gather(half, "blk", axis=1, tiled=True)
    square = fold_product(row_block, half)
    cube = fold_product(row_block, square.astype(jnp.bfloat16))
    return 4.0 * identity - 6.0 * scaled + 4.0 * square - cube


def tiled_body(activations, out_grads):
    tok_count = lax.axis_size("tok")
    blk_count = lax.axis_size("blk")
    tok_id = lax.axis_index("tok")
    blk_id = lax.axis_index("blk")
    token_count = activations.shape[0] * tok_count
    tile_cols = activations.shape[1]
    tile_rows = tile_cols * blk_count // tok_count
    row_ids = tok_id * tile_rows + jnp.arange(tile_rows, dtype=jnp.int32)
    col_ids = blk_id * tile_cols + jnp.arange(tile_cols, dtype=jnp.int32)
    identity = (row_ids[:, None] == col_ids[None, :]).astype(jnp.float32)

    def inverse_tile(local):
        full = lax.all_gather(local, "blk", axis=1, tiled=True)
        sums = lax.psum(column_squares(full).astype(jnp.bfloat16), "tok").astype(jnp.float32)
        gram_tile = lax.psum_scatter(
            lax.dot_general(
                full, local, (((0,), (0,)), ((), ())), preferred_element_type=jnp.float32
            ).astype(jnp.bfloat16),
            "tok",
            scatter_dimension=0,
            tiled=True,
        ).astype(jnp.float32)
        inverse = lax.rsqrt(sums / token_count + epsilon)
        inverse_rows = lax.dynamic_slice_in_dim(inverse, tok_id * tile_rows, tile_rows)
        inverse_cols = lax.dynamic_slice_in_dim(inverse, blk_id * tile_cols, tile_cols)
        damped = (
            gram_tile / token_count * inverse_rows[:, None] * inverse_cols[None, :]
            + damping * identity
        )
        result_tile = newton_steps(damped / divisor, identity)
        return lax.all_to_all(
            result_tile.astype(jnp.bfloat16), "blk", split_axis=0, concat_axis=1, tiled=True
        ).astype(result_tile.dtype)

    return inverse_tile(activations), inverse_tile(out_grads)


def cut(length, unit, pieces):
    units = length // unit
    sizes = [(units // pieces + (1 if i < units % pieces else 0)) * unit for i in range(pieces)]
    return [(sum(sizes[:i]), sizes[i]) for i in range(pieces)]


def gather_kernel(tok, blk, swaps, block_shape, *refs):
    first, second, out, send_sem, recv_sem, pass_send, pass_recv, swap_send, swap_recv, local_sem = refs
    t = lax.axis_index("tok")
    b = lax.axis_index("blk")
    half = blk // 2
    dims = []
    bit = 2
    while bit < tok:
        dims.append((bit, 0))
        bit *= 2
    bit = 1
    while bit < half:
        dims.append((0, bit))
        bit *= 2
    count = len(dims)
    rows, cols = block_shape
    if swaps:
        parts = [((o, n), (0, cols)) for o, n in cut(rows, 16, count)]
    else:
        parts = [((0, rows), (o, n)) for o, n in cut(cols, 128, count)]

    def flip(j, steps, tok_bits=0, blk_bits=0):
        for s in range(count):
            if steps >> s & 1:
                dt, db = dims[(j + s) % count]
                tok_bits ^= dt
                blk_bits ^= db
        return jnp.bitwise_xor(t, tok_bits), jnp.bitwise_xor(b, blk_bits)

    def place(q, part, owner):
        (r0, rn), (c0, cn) = parts[part]
        tt, bb = owner
        if q:
            bb = jnp.bitwise_xor(bb, half)
        if swaps:
            row, col = tt * rows + r0, bb * cols + c0
        else:
            row, col = (tt * blk + bb) * rows + r0, c0
        return out.at[
            pl.ds(pl.multiple_of(row, 16), rn), pl.ds(pl.multiple_of(col, 128), cn)
        ]

    def own(q, part):
        (r0, rn), (c0, cn) = parts[part]
        if q and swaps:
            return place(q, part, (t, b))
        return (second if q else first).at[pl.ds(r0, rn), pl.ds(c0, cn)]

    def hop(q, j, steps, s):
        src = own(q, j) if steps == 0 else place(q, j, flip(j, steps))
        index = (q * count + j) * 2**count + (steps | 1 << s)
        return pltpu.make_async_remote_copy(
            src_ref=src,
            dst_ref=place(q, j, flip(j, steps)),
            send_sem=send_sem.at[index],
            recv_sem=recv_sem.at[index],
            device_id=flip(j, 1 << s),
            device_id_type=MESH,
        )

    def arrival(q, j, steps):
        index = (q * count + j) * 2**count + steps
        where = place(q, j, flip(j, steps))
        return pltpu.make_async_remote_copy(
            src_ref=where,
            dst_ref=where,
            send_sem=send_sem.at[index],
            recv_sem=recv_sem.at[index],
            device_id=flip(j, 1),
            device_id_type=MESH,
        )

    def handed(q, j, steps, sender):
        index = (q * count + j) * 2**count + steps
        if sender:
            where = place(q, j, flip(j, steps))
            src = own(q, j) if steps == 0 else where
        else:
            where = place(q, j, flip(j, steps, 1))
            src = where
        return pltpu.make_async_remote_copy(
            src_ref=src,
            dst_ref=where,
            send_sem=pass_send.at[index],
            recv_sem=pass_recv.at[index],
            device_id=(jnp.bitwise_xor(t, 1), b),
            device_id_type=MESH,
        )

    across = (t, jnp.bitwise_xor(b, half))

    def swap(part, sender):
        (r0, rn), (c0, cn) = parts[part]
        if sender:
            src = second.at[pl.ds(r0, rn), pl.ds(c0, cn)]
            where = place(1, part, across)
        else:
            src = where = place(1, part, (t, b))
        return pltpu.make_async_remote_copy(
            src_ref=src,
            dst_ref=where,
            send_sem=swap_send.at[part],
            recv_sem=swap_recv.at[part],
            device_id=across,
            device_id_type=MESH,
        )

    barrier = pltpu.get_barrier_semaphore()
    peers = [flip(0, 1 << s) for s in range(count)] + [(jnp.bitwise_xor(t, 1), b)]
    if swaps:
        peers.append(across)
    for peer in peers:
        pl.semaphore_signal(barrier, inc=1, device_id=peer, device_id_type=MESH)
    pl.semaphore_wait(barrier, len(peers))

    pending = []

    def start(copy):
        copy.start()
        pending.append(copy)

    def begin(q):
        for s in range(count):
            for j in range(count):
                if s == 0 and q and swaps:
                    swap(j, False).wait_recv()
                start(hop(q, j, 0, s))
        for j in range(count):
            start(handed(q, j, 0, True))

    def advance(q, p):
        for steps in range(2**p, 2 ** (p + 1)):
            for j in range(count):
                arrival(q, j, steps).wait_recv()
                for s in range(p + 1, count):
                    start(hop(q, j, steps, s))
                start(handed(q, j, steps, True))

    begin(0)
    if swaps:
        for part in range(count):
            start(swap(part, True))
    locals_ = []
    for q in range(1 if swaps else 2):
        for part in range(count):
            copy = pltpu.make_async_copy(
                own(q, part), place(q, part, (t, b)), local_sem.at[q * count + part]
            )
            copy.start()
            locals_.append(copy)
    for p in range(count - 1):
        advance(0, p)
    begin(1)
    advance(0, count - 1)
    for p in range(count):
        advance(1, p)
    for q in range(2):
        for j in range(count):
            for steps in range(2**count):
                handed(q, j, steps, False).wait_recv()
    for copy in locals_:
        copy.wait()
    for copy in pending:
        copy.wait_send()


def gather(first, second, tok, blk, swaps, full_shape, collective_id):
    count = (tok // 2).bit_length() - 1 + (blk // 2).bit_length() - 1
    slots = 2 * count * 2**count
    return pl.pallas_call(
        functools.partial(gather_kernel, tok, blk, swaps, first.shape),
        out_shape=jax.ShapeDtypeStruct(full_shape, first.dtype),
        in_specs=[pl.BlockSpec(memory_space=pltpu.VMEM)] * 2,
        out_specs=pl.BlockSpec(memory_space=pl.ANY),
        scratch_shapes=[pltpu.SemaphoreType.DMA((slots,))] * 4
        + [pltpu.SemaphoreType.DMA((count,))] * 2
        + [pltpu.SemaphoreType.DMA((2 * count,))],
        compiler_params=pltpu.CompilerParams(
            collective_id=collective_id, has_side_effects=True, vmem_limit_bytes=16 * 1024 * 1024
        ),
        cost_estimate=pl.CostEstimate(
            flops=0, bytes_accessed=2 * full_shape[0] * full_shape[1] * 16, transcendentals=0
        ),
    )(first, second)


def split_body(tok, blk, activations, out_grads):
    half = blk // 2
    t = lax.axis_index("tok")
    b = lax.axis_index("blk")
    tokens = activations.shape[0] * tok
    width = activations.shape[1] * blk
    rows = width // (tok * blk)
    low = b < half
    mine = jnp.where(low, activations, out_grads)
    other = jnp.where(low, out_grads, activations)

    partial_sums = jnp.stack([column_squares(activations), column_squares(out_grads)])
    all_sums = lax.all_gather(partial_sums, ("tok", "blk"), axis=0, tiled=False)
    both = all_sums.reshape(tok, blk, 2, -1).sum(axis=0).transpose(1, 0, 2).reshape(2, width)
    sums = jnp.where(low, both[0], both[1])
    inverse = lax.rsqrt(sums / tokens + epsilon)

    x = gather(mine, other, tok, blk, True, (tokens, width), 0)
    starts = [(t * blk + b) * rows, (t * blk + jnp.bitwise_xor(b, half)) * rows]
    x_own = jnp.concatenate(
        [lax.dynamic_slice_in_dim(x, s, rows, axis=1) for s in starts], axis=1
    )
    inverse_own = jnp.concatenate([lax.dynamic_slice_in_dim(inverse, s, rows) for s in starts])
    gram = lax.dot_general(x_own, x, (((0,), (0,)), ((), ())), preferred_element_type=jnp.float32)
    row_ids = jnp.concatenate([s + jnp.arange(rows, dtype=jnp.int32) for s in starts])
    identity = (row_ids[:, None] == jnp.arange(width, dtype=jnp.int32)[None, :]).astype(jnp.float32)
    scaled = (
        gram / tokens * inverse_own[:, None] * inverse[None, :] + damping * identity
    ) / divisor
    h_own = scaled.astype(jnp.bfloat16)
    h = gather(h_own[:rows], h_own[rows:], tok, blk, False, (width, width), 1)
    square = jnp.dot(h_own, h, preferred_element_type=jnp.float32)
    cube = jnp.dot(square.astype(jnp.bfloat16), h, preferred_element_type=jnp.float32)
    result = 4.0 * identity - 6.0 * scaled + 4.0 * square - cube
    kept = result[:rows]
    came = lax.ppermute(
        result[rows:].astype(jnp.bfloat16), "blk", [(i, i ^ half) for i in range(blk)]
    ).astype(jnp.float32)
    return jnp.where(low, kept, came), jnp.where(low, came, kept)


def solution(mesh):
    tok, blk = mesh.shape["tok"], mesh.shape["blk"]
    placed = (P("tok", "blk"), P("tok", "blk"))

    def body(activations, out_grads):
        tokens, width = activations.shape[0] * tok, activations.shape[1] * blk
        whole = max(tokens, width) * width * activations.dtype.itemsize
        powers = tok & (tok - 1) == 0 and blk & (blk - 1) == 0 and tok > 2 and blk > 1
        if whole <= gathered_budget and powers:
            return split_body(tok, blk, activations, out_grads)
        return tiled_body(activations, out_grads)

    return jax.shard_map(
        body,
        mesh=mesh,
        in_specs=placed,
        out_specs=(P(("tok", "blk"), None), P(("tok", "blk"), None)),
        check_vma=False,
    )
```

time: 764 us -> 460 us (0.60)
  waiting for transfers between devices: 641 us -> 48.9 us
  Pallas kernels: 0 us -> 249 us
  blocking collectives: 24.5 us -> 72 us
  local copies, waits for them, and re-layouts: 4 us -> 25.7 us
  between operations: 14.3 us -> 0.75 us
  starting transfers between devices: 9.9 us -> 0.07 us
    all_gather x8 -> x0, waiting for transfers between devices: 504 us -> none  [the longest x4 197 us: fold_product(): lax.all_gather(tile, 'tok', axis=0, tiled=True)]
    pallas_call x0 -> x2, Pallas kernels: none -> 249 us  [gather(): pl.pallas_call(functools.partial(gather_kernel, tok, blk, swaps, first.sh...]
    reduce_scatter x2 -> x0, waiting for transfers between devices: 109 us -> none  [damped_tile(): lax.psum_scatter(lax.dot_general(full, local, (((0,), (0,)), ((), ())), p...]
    all_gather x0 -> x1, blocking collectives: none -> 72 us  [split_body(): all_sums = lax.all_gather(partial_sums, ('tok', 'blk'), axis=0, tiled=False)]
    ppermute x0 -> x1, waiting for transfers between devices: none -> 48.9 us  [split_body(): lax.ppermute(result[rows:].astype(jnp.bfloat16), 'blk', [(i, i ^ half) fo...]
    psum x1 -> x0, blocking collectives: 24.5 us -> none  [body(): lax.psum(column_squares(full_acts).astype(jnp.bfloat16), 'tok')]
    all_to_all x2 -> x0, waiting for transfers between devices: 24.4 us -> none  [body(): lax.all_to_all(result_tile.astype(jnp.bfloat16), 'blk', split_axis=0, con...]
    unnamed x10 -> x4, local copies, waits for them, and re-layouts: 1.05 us -> 22.1 us
  transfers between devices with their start and end apart: 12 -> 1, of which waited for: 11 -> 1; matrix products, arithmetic and copies ran while one was open for 9% -> 0% of each run, Pallas kernels for 0% -> 0%
where the time goes in v1:
time: 460 us
  Pallas kernels  249 us (54%)
  blocking collectives  72 us (16%)
  matrix products  54.1 us (12%)
  waiting for transfers between devices  48.9 us (11%)
  local copies, waits for them, and re-layouts  25.7 us (6%)
  other arithmetic  8.88 us (2%)
    pallas_call x2, Pallas kernels, gather(): pl.pallas_call(functools.partial(gather_kernel, tok, blk, swaps, first.sh...  249 us
    all_gather x1, blocking collectives, split_body(): all_sums = lax.all_gather(partial_sums, ('tok', 'blk'), axis=0, tiled=False)  72 us
    ppermute x1, waiting for transfers between devices, split_body(): lax.ppermute(result[rows:].astype(jnp.bfloat16), 'blk', [(i, i ^ half) fo...  48.9 us
    unnamed x4, local copies, waits for them, and re-layouts  22.1 us
    dot_general x1, matrix products, split_body(): jnp.dot(square.astype(jnp.bfloat16), h, preferred_element_type=jnp.float32)  20.2 us
    dot_general x1, matrix products, split_body(): square = jnp.dot(h_own, h, preferred_element_type=jnp.float32)  17 us
    dot_general x1, matrix products, split_body(): lax.dot_general(x_own, x, (((0,), (0,)), ((), ())), preferred_element_typ...  16.8 us
  transfers between devices with their start and end apart: 1, of which 1 were waited for; matrix products, arithmetic and copies ran while one was open for 0% of the time, Pallas kernels for 0%

profile of v1, /device:TPU:0, one launch (start us, length us, event | category | flops | bytes accessed | tf_op | source)
XLA Modules:
  0.0 459.5 jit_solution(11499050217324309735)
XLA Ops:
  0.7 1.5 multiply_reduce_fusion.1
  2.1 1.5 multiply_reduce_fusion
  3.6 72.0 %all-gather.1 = f32[32,2,1024]{2,1,0:T(2,128)S(1)} all-gather(f32[1,2,1024]{2,1,0:T(2,128)S(1)} %maximum_bitcast_fusion), channel_id=2, replica_groups=mesh['tok'=8,'blk'=4] {'tok','blk'}, dimensions={0}, use_global_device_ids=true | all-gather | bytes 270336 | tf_op jit(solution)/shard_map/all_gather | solution.py:280
  75.6 1.7 broadcast_select_fusion
  77.3 0.1 reduce_sum.29
  77.4 132.0 %shard_map.41 = bf16[4096,4096]{1,0:T(8,128)(2,1)S(1)} custom-call(bf16[512,1024]{1,0:T(8,128)(2,1)S(1)} %get-tuple-element.9.refs_0_, bf16[512,1024]{1,0:T(8,128)(2,1)S(1)} %get-tuple-element.8.refs_1_), custom_call_target="tpu_custom_call" | custom-call | bytes 536870912 | tf_op jit(solution)/shard_map/pallas_call | solution.py:251
  209.4 0.0 copy-start
  209.4 11.1 %copy-done = bf16[4096,4096]{1,0:T(8,128)(2,1)} copy-done((bf16[4096,4096]{1,0:T(8,128)(2,1)}, bf16[4096,4096]{1,0:T(8,128)(2,1)S(1)}, u32[]{:S(2)}) %copy-start) | copy-done | bytes 33554456
  220.5 0.1 fusion.11
  220.6 1.7 constant_dynamic-slice_fusion.1
  222.3 16.8 %multiply_convert_fusion = (bf16[256,4096]{1,0:T(8,128)(2,1)S(1)}, f32[256,4096]{1,0:T(8,128)}) fusion(s32[256]{0:T(256)S(1)} %pad_add_fusion, f32[4096]{0:T(1024)S(1)} %bitcast.14, f32[256]{0:T(256)S(1)} %maximum_multiply_fusion, bf16[4096,4096]{1,0:T(8,128)(2,1)} %copy-done, bf16[4096,128]{1,0:T(8,128)(2,1)S(1)} %get-tuple-element.3, ...), kind=kOutput, calls=%fused_computation.4 | convolution fusion | flops 8601468928 | bytes 41961472 | tf_op jit(solution)/shard_map/dot_general | solution.py:291
  239.1 0.1 fusion.10
  239.2 117.1 %shard_map.42 = bf16[4096,4096]{1,0:T(8,128)(2,1)S(1)} custom-call(bf16[128,4096]{1,0:T(8,128)(2,1)S(1)} %get-tuple-element.7.refs_0_, bf16[128,4096]{1,0:T(8,128)(2,1)S(1)} %get-tuple-element.6.refs_1_), custom_call_target="tpu_custom_call" | custom-call | bytes 536870912 | tf_op jit(solution)/shard_map/pallas_call | solution.py:251
  356.4 0.0 copy-start.1
  356.4 11.1 %copy-done.1 = bf16[4096,4096]{1,0:T(8,128)(2,1)} copy-done((bf16[4096,4096]{1,0:T(8,128)(2,1)}, bf16[4096,4096]{1,0:T(8,128)(2,1)S(1)}, u32[]{:S(2)}) %copy-start.1) | copy-done | bytes 33554456
  367.4 17.0 %fusion.12 = f32[256,4096]{1,0:T(8,128)} fusion(bf16[256,4096]{1,0:T(8,128)(2,1)S(1)} %get-tuple-element.12, bf16[4096,4096]{1,0:T(8,128)(2,1)} %copy-done.1), kind=kOutput, calls=%fused_computation.31 | convolution fusion | flops 8589934592 | bytes 39845888 | tf_op jit(solution)/shard_map/dot_general | solution.py:299
  384.5 20.2 %convolution_subtract_fusion = f32[256,4096]{1,0:T(8,128)} fusion(bf16[4096,4096]{1,0:T(8,128)(2,1)} %copy-done.1, f32[256,4096]{1,0:T(8,128)} %fusion.12, f32[256,4096]{1,0:T(8,128)} %get-tuple-element.13, s32[256]{0:T(256)S(1)} %pad_add_fusion), kind=kOutput, calls=%fused_computation.2 | convolution fusion | flops 8598323200 | bytes 46138368 | tf_op jit(solution)/shard_map/dot_general | solution.py:300
  404.7 1.7 slice.42
  406.4 0.1 collective-permute-start
  406.5 48.9 %collective-permute-done = bf16[128,4096]{1,0:T(8,128)(2,1)S(1)} collective-permute-done((bf16[128,4096]{1,0:T(8,128)(2,1)S(1)}, bf16[128,4096]{1,0:T(8,128)(2,1)S(1)}, u32[]{:S(2)}, u32[]{:S(2)}) %collective-permute-start) | collective-permute-done | bytes 1048608 | tf_op jit(solution)/shard_map/ppermute | solution.py:303
  455.4 4.1 convert_select_fusion
  (5 shorter events, 0.1 us)
Async XLA Ops:
  209.4 11.1 %copy-start = (bf16[4096,4096]{1,0:T(8,128)(2,1)}, bf16[4096,4096]{1,0:T(8,128)(2,1)S(1)}, u32[]{:S(2)}) copy-start(bf16[4096,4096]{1,0:T(8,128)(2,1)S(1)} %shard_map.41) | copy-start | bytes 100663296
  356.4 11.1 %copy-start.1 = (bf16[4096,4096]{1,0:T(8,128)(2,1)}, bf16[4096,4096]{1,0:T(8,128)(2,1)S(1)}, u32[]{:S(2)}) copy-start(bf16[4096,4096]{1,0:T(8,128)(2,1)S(1)} %shard_map.42) | copy-start | bytes 100663296
  406.4 49.0 %collective-permute-start = (bf16[128,4096]{1,0:T(8,128)(2,1)S(1)}, bf16[128,4096]{1,0:T(8,128)(2,1)S(1)}, u32[]{:S(2)}, u32[]{:S(2)}) collective-permute-start(bf16[128,4096]{1,0:T(8,128)(2,1)S(1)} %slice.42), channel_id=1, source_target_pairs={{0,2},{1,3},{2,0},{3,1},{4,6},{5,7},{6,4},{7,5},{8,10},{9,11},{10,... | collective-permute-start | bytes 3145736 | tf_op jit(solution)/shard_map/ppermute | solution.py:303

commit v2 on v1

--- a/solution.py
+++ b/solution.py
@@ -11,6 +11,8 @@
 epsilon = 1e-06
 divisor = 2.0
 gathered_budget = 32 * 1024 * 1024
+LANES = 128
+CHUNK = 512
 MESH = pl.DeviceIdType.MESH
 
 
@@ -79,8 +81,8 @@
     return [(sum(sizes[:i]), sizes[i]) for i in range(pieces)]
 
 
-def gather_kernel(tok, blk, swaps, block_shape, *refs):
-    first, second, out, send_sem, recv_sem, pass_send, pass_recv, swap_send, swap_recv, local_sem = refs
+def gather_blocks(tok, blk, swaps, first, second, out, sems):
+    send_sem, recv_sem, pass_send, pass_recv, swap_send, swap_recv, local_sem = sems
     t = lax.axis_index("tok")
     b = lax.axis_index("blk")
     half = blk // 2
@@ -94,7 +96,7 @@
         dims.append((0, bit))
         bit *= 2
     count = len(dims)
-    rows, cols = block_shape
+    rows, cols = first.shape
     if swaps:
         parts = [((o, n), (0, cols)) for o, n in cut(rows, 16, count)]
     else:
@@ -187,9 +189,7 @@
         )
 
     barrier = pltpu.get_barrier_semaphore()
-    peers = [flip(0, 1 << s) for s in range(count)] + [(jnp.bitwise_xor(t, 1), b)]
-    if swaps:
-        peers.append(across)
+    peers = [flip(0, 1 << s) for s in range(count)] + [(jnp.bitwise_xor(t, 1), b), across]
     for peer in peers:
         pl.semaphore_signal(barrier, inc=1, device_id=peer, device_id_type=MESH)
     pl.semaphore_wait(barrier, len(peers))
@@ -245,64 +245,190 @@
         copy.wait_send()
 
 
-def gather(first, second, tok, blk, swaps, full_shape, collective_id):
+def gather_scratch(tok, blk):
     count = (tok // 2).bit_length() - 1 + (blk // 2).bit_length() - 1
     slots = 2 * count * 2**count
-    return pl.pallas_call(
-        functools.partial(gather_kernel, tok, blk, swaps, first.shape),
-        out_shape=jax.ShapeDtypeStruct(full_shape, first.dtype),
-        in_specs=[pl.BlockSpec(memory_space=pltpu.VMEM)] * 2,
-        out_specs=pl.BlockSpec(memory_space=pl.ANY),
-        scratch_shapes=[pltpu.SemaphoreType.DMA((slots,))] * 4
+    return (
+        [pltpu.SemaphoreType.DMA((slots,))] * 4
         + [pltpu.SemaphoreType.DMA((count,))] * 2
-        + [pltpu.SemaphoreType.DMA((2 * count,))],
-        compiler_params=pltpu.CompilerParams(
-            collective_id=collective_id, has_side_effects=True, vmem_limit_bytes=16 * 1024 * 1024
-        ),
-        cost_estimate=pl.CostEstimate(
-            flops=0, bytes_accessed=2 * full_shape[0] * full_shape[1] * 16, transcendentals=0
-        ),
-    )(first, second)
-
-
-def split_body(tok, blk, activations, out_grads):
-    half = blk // 2
+        + [pltpu.SemaphoreType.DMA((2 * count,))]
+    )
+
+
+def row_starts(tok, blk, rows):
     t = lax.axis_index("tok")
     b = lax.axis_index("blk")
+    return [
+        pl.multiple_of((t * blk + bb) * rows, LANES) for bb in (b, jnp.bitwise_xor(b, blk // 2))
+    ]
+
+
+def gram_kernel(tok, blk, first, second, gram, rounded, x, turned, *sems):
+    tokens, width = x.shape
+    rows = width // (tok * blk)
+    gather_blocks(tok, blk, True, first, second, x, sems)
+    step = first.shape[0]
+    for s, start in enumerate(row_starts(tok, blk, rows)):
+
+        @pl.loop(0, tokens // step)
+        def _(i):
+            at = pl.ds(pl.multiple_of(i * step, step), step)
+            turned[s * rows : (s + 1) * rows, at] = x[at, pl.ds(start, rows)].T
+
+    @pl.loop(0, width // CHUNK)
+    def _(i):
+        at = pl.ds(pl.multiple_of(i * CHUNK, CHUNK), CHUNK)
+        product = jnp.dot(turned[...], x[:, at], preferred_element_type=jnp.float32)
+        gram[:, at] = product
+        rounded[:, at] = product.astype(jnp.bfloat16)
+
+
+def newton_kernel(
+    tok, blk, tokens, first, second, gram, kept, came, g, square, left, inverse, sent,
+    out_sem, in_sem, *sems
+):
+    width = g.shape[1]
+    rows = width // (tok * blk)
+    t = lax.axis_index("tok")
+    b = lax.axis_index("blk")
+    starts = row_starts(tok, blk, rows)
+    gather_blocks(tok, blk, False, first, second, g, sems)
+    factor = 1.0 / (tokens * divisor)
+    shift = damping / divisor
+    eye = lax.broadcasted_iota(jnp.int32, (LANES, LANES), 0) == lax.broadcasted_iota(
+        jnp.int32, (LANES, LANES), 1
+    )
+
+    @pl.loop(0, width // LANES)
+    def _(i):
+        at = pl.ds(pl.multiple_of(i * LANES, LANES), LANES)
+        block = jnp.where(eye, g[at, at].astype(jnp.float32), 0.0)
+        inverse[:, at] = lax.rsqrt(jnp.sum(block, axis=0, keepdims=True) / tokens + epsilon)
+
+    inverse_rows = []
+    for s, start in enumerate(starts):
+        parts = []
+        for r in range(0, rows, LANES):
+            own = gram[s * rows + r : s * rows + r + LANES, pl.ds(start + r, LANES)]
+            total = jnp.sum(jnp.where(eye, own, 0.0), axis=1, keepdims=True)
+            parts.append(lax.rsqrt(total / tokens + epsilon))
+        inverse_rows += parts
+    inverse_rows = jnp.concatenate(inverse_rows, axis=0)
+
+    def identity(i):
+        col = i * CHUNK + lax.broadcasted_iota(jnp.int32, (rows, CHUNK), 1)
+        row = lax.broadcasted_iota(jnp.int32, (rows, CHUNK), 0)
+        return jnp.concatenate(
+            [(col - start == row).astype(jnp.float32) for start in starts], axis=0
+        )
+
+    def scaled(i, at):
+        return gram[:, at] * factor * inverse_rows * inverse[:, at] + shift * identity(i)
+
+    @pl.loop(0, width // CHUNK)
+    def _(i):
+        at = pl.ds(pl.multiple_of(i * CHUNK, CHUNK), CHUNK)
+        left[:, at] = (scaled(i, at) * inverse[:, at]).astype(jnp.bfloat16)
+
+    @pl.loop(0, width // CHUNK)
+    def _(i):
+        at = pl.ds(pl.multiple_of(i * CHUNK, CHUNK), CHUNK)
+        product = jnp.dot(left[...], g[:, at], preferred_element_type=jnp.float32)
+        square[:, at] = product * (inverse[:, at] * factor) + shift * scaled(i, at)
+
+    @pl.loop(0, width // CHUNK)
+    def _(i):
+        at = pl.ds(pl.multiple_of(i * CHUNK, CHUNK), CHUNK)
+        left[:, at] = (square[:, at] * inverse[:, at]).astype(jnp.bfloat16)
+
+    def swap(i):
+        at = pl.ds(pl.multiple_of(i * CHUNK, CHUNK), CHUNK)
+        return pltpu.make_async_remote_copy(
+            src_ref=sent.at[:, at],
+            dst_ref=came.at[:, at],
+            send_sem=out_sem.at[i],
+            recv_sem=in_sem.at[i],
+            device_id=(t, jnp.bitwise_xor(b, blk // 2)),
+            device_id_type=MESH,
+        )
+
+    steps = width // CHUNK
+
+    def finish(i):
+        at = pl.ds(pl.multiple_of(i * CHUNK, CHUNK), CHUNK)
+        product = jnp.dot(left[...], g[:, at], preferred_element_type=jnp.float32)
+        squared = square[:, at]
+        cube = product * (inverse[:, at] * factor) + shift * squared
+        result = 4.0 * identity(i) - 6.0 * scaled(i, at) + 4.0 * squared - cube
+        kept[:, at] = result[:rows]
+        sent[:, at] = result[rows:].astype(jnp.bfloat16)
+
+    finish(0)
+
+    @pl.loop(1, steps)
+    def _(i):
+        finish(i)
+        swap(i - 1).start()
+
+    swap(steps - 1).start()
+
+    @pl.loop(0, steps)
+    def _(i):
+        swap(i).wait_recv()
+        swap(i).wait_send()
+
+
+def call(kernel, outs, scratch, tok, blk, collective_id, *operands):
+    return pl.pallas_call(
+        kernel,
+        out_shape=outs,
+        in_specs=[pl.BlockSpec(memory_space=pltpu.VMEM)] * len(operands),
+        out_specs=[pl.BlockSpec(memory_space=pltpu.VMEM)] * len(outs),
+        scratch_shapes=scratch + gather_scratch(tok, blk),
+        compiler_params=pltpu.CompilerParams(
+            collective_id=collective_id, has_side_effects=True, vmem_limit_bytes=60 * 1024 * 1024
+        ),
+    )(*operands)
+
+
+def split_body(tok, blk, activations, out_grads):
     tokens = activations.shape[0] * tok
     width = activations.shape[1] * blk
     rows = width // (tok * blk)
-    low = b < half
+    low = lax.axis_index("blk") < blk // 2
     mine = jnp.where(low, activations, out_grads)
     other = jnp.where(low, out_grads, activations)
-
-    partial_sums = jnp.stack([column_squares(activations), column_squares(out_grads)])
-    all_sums = lax.all_gather(partial_sums, ("tok", "blk"), axis=0, tiled=False)
-    both = all_sums.reshape(tok, blk, 2, -1).sum(axis=0).transpose(1, 0, 2).reshape(2, width)
-    sums = jnp.where(low, both[0], both[1])
-    inverse = lax.rsqrt(sums / tokens + epsilon)
-
-    x = gather(mine, other, tok, blk, True, (tokens, width), 0)
-    starts = [(t * blk + b) * rows, (t * blk + jnp.bitwise_xor(b, half)) * rows]
-    x_own = jnp.concatenate(
-        [lax.dynamic_slice_in_dim(x, s, rows, axis=1) for s in starts], axis=1
-    )
-    inverse_own = jnp.concatenate([lax.dynamic_slice_in_dim(inverse, s, rows) for s in starts])
-    gram = lax.dot_general(x_own, x, (((0,), (0,)), ((), ())), preferred_element_type=jnp.float32)
-    row_ids = jnp.concatenate([s + jnp.arange(rows, dtype=jnp.int32) for s in starts])
-    identity = (row_ids[:, None] == jnp.arange(width, dtype=jnp.int32)[None, :]).astype(jnp.float32)
-    scaled = (
-        gram / tokens * inverse_own[:, None] * inverse[None, :] + damping * identity
-    ) / divisor
-    h_own = scaled.astype(jnp.bfloat16)
-    h = gather(h_own[:rows], h_own[rows:], tok, blk, False, (width, width), 1)
-    square = jnp.dot(h_own, h, preferred_element_type=jnp.float32)
-    cube = jnp.dot(square.astype(jnp.bfloat16), h, preferred_element_type=jnp.float32)
-    result = 4.0 * identity - 6.0 * scaled + 4.0 * square - cube
-    kept = result[:rows]
-    came = lax.ppermute(
-        result[rows:].astype(jnp.bfloat16), "blk", [(i, i ^ half) for i in range(blk)]
-    ).astype(jnp.float32)
+    steps = width // CHUNK
+    gram, rounded = call(
+        functools.partial(gram_kernel, tok, blk),
+        [
+            jax.ShapeDtypeStruct((2 * rows, width), jnp.float32),
+            jax.ShapeDtypeStruct((2 * rows, width), jnp.bfloat16),
+        ],
+        [
+            pltpu.VMEM((tokens, width), jnp.bfloat16),
+            pltpu.VMEM((2 * rows, tokens), jnp.bfloat16),
+        ],
+        tok, blk, 0, mine, other,
+    )
+    kept, came = call(
+        functools.partial(newton_kernel, tok, blk, tokens),
+        [
+            jax.ShapeDtypeStruct((rows, width), jnp.float32),
+            jax.ShapeDtypeStruct((rows, width), jnp.bfloat16),
+        ],
+        [
+            pltpu.VMEM((width, width), jnp.bfloat16),
+            pltpu.VMEM((2 * rows, width), jnp.float32),
+            pltpu.VMEM((2 * rows, width), jnp.bfloat16),
+            pltpu.VMEM((1, width), jnp.float32),
+            pltpu.VMEM((rows, width), jnp.bfloat16),
+            pltpu.SemaphoreType.DMA((steps,)),
+            pltpu.SemaphoreType.DMA((steps,)),
+        ],
+        tok, blk, 1, rounded[:rows], rounded[rows:], gram,
+    )
+    came = came.astype(jnp.float32)
     return jnp.where(low, kept, came), jnp.where(low, came, kept)
 
 
@@ -314,6 +440,7 @@
         tokens, width = activations.shape[0] * tok, activations.shape[1] * blk
         whole = max(tokens, width) * width * activations.dtype.itemsize
         powers = tok & (tok - 1) == 0 and blk & (blk - 1) == 0 and tok > 2 and blk > 1
+        powers = powers and width % (tok * blk * LANES) == 0
         if whole <= gathered_budget and powers:
             return split_body(tok, blk, activations, out_grads)
         return tiled_body(activations, out_grads)

time: 460 us -> 349 us (0.76)
  Pallas kernels: 249 us -> 338 us
  blocking collectives: 72 us -> 0 us
  matrix products: 54.1 us -> 0 us
  waiting for transfers between devices: 48.9 us -> 0 us
  local copies, waits for them, and re-layouts: 25.7 us -> 3.08 us
    pallas_call x2, Pallas kernels: 249 us -> 338 us  [call(): pl.pallas_call(kernel, out_shape=outs, in_specs=[pl.BlockSpec(memory_spac...]
    all_gather x1 -> x0, blocking collectives: 72 us -> none  [split_body(): all_sums = lax.all_gather(partial_sums, ('tok', 'blk'), axis=0, tiled=False)]
    dot_general x3 -> x0, matrix products: 54.1 us -> none  [the longest x1 20.2 us: split_body(): jnp.dot(square.astype(jnp.bfloat16), h, preferred_element_type=jnp.float32)]
    ppermute x1 -> x0, waiting for transfers between devices: 48.9 us -> none  [split_body(): lax.ppermute(result[rows:].astype(jnp.bfloat16), 'blk', [(i, i ^ half) fo...]
    unnamed x4 -> x0, local copies, waits for them, and re-layouts: 22.1 us -> none
  transfers between devices with their start and end apart: 1 -> 0, of which waited for: 1 -> 0; matrix products, arithmetic and copies ran while one was open for 0% -> 0% of each run, Pallas kernels for 0% -> 0%
where the time goes in v2:
time: 349 us
  Pallas kernels  338 us (97%)
  other arithmetic  7.37 us (2%)
    pallas_call x2, Pallas kernels, call(): pl.pallas_call(kernel, out_shape=outs, in_specs=[pl.BlockSpec(memory_spac...  338 us

profile of v2, /device:TPU:0, one launch (start us, length us, event | category | flops | bytes accessed | tf_op | source)
XLA Modules:
  0.0 348.9 jit_solution(3700161277574670120)
XLA Ops:
  0.6 3.0 broadcast_select_fusion
  3.6 155.1 %shard_map.41 = (f32[256,4096]{1,0:T(8,128)}, bf16[256,4096]{1,0:T(8,128)(2,1)}) custom-call(bf16[512,1024]{1,0:T(8,128)(2,1)} %get-tuple-element.15.first, bf16[512,1024]{1,0:T(8,128)(2,1)} %get-tuple-element.14.second), custom_call_target="tpu_custom_call" | custom-call | tf_op jit(solution)/shard_map/pallas_call | solution.py:382
  158.7 3.1 fusion
  161.8 182.7 %shard_map.42 = (f32[128,4096]{1,0:T(8,128)}, bf16[128,4096]{1,0:T(8,128)(2,1)}) custom-call(bf16[128,4096]{1,0:T(8,128)(2,1)} %get-tuple-element.13.first, bf16[128,4096]{1,0:T(8,128)(2,1)} %get-tuple-element.12.second, f32[256,4096]{1,0:T(8,128)} %get-tuple-element.7.gram), custom_call_target="tpu_custom_call" | custom-call | tf_op jit(solution)/shard_map/pallas_call | solution.py:382
  344.5 4.4 %convert_select_fusion = (f32[128,4096]{1,0:T(8,128)}, f32[128,4096]{1,0:T(8,128)}) fusion(f32[128,4096]{1,0:T(8,128)} %get-tuple-element.8, bf16[128,4096]{1,0:T(8,128)(2,1)} %get-tuple-element.9, pred[]{:T(512)S(6)} %lt.3), kind=kLoop, calls=%fused_computation | loop fusion | flops 1572864 | bytes 7340033 | tf_op jit(solution)/shard_map/jit(_where)/select_n | solution.py:432

commit v3 on v2

--- a/solution.py
+++ b/solution.py
@@ -2,6 +2,7 @@
 
 import jax
 import jax.numpy as jnp
+import numpy as np
 from jax import lax
 from jax.experimental import pallas as pl
 from jax.experimental.pallas import tpu as pltpu
@@ -81,7 +82,16 @@
     return [(sum(sizes[:i]), sizes[i]) for i in range(pieces)]
 
 
-def gather_blocks(tok, blk, swaps, first, second, out, sems):
+def swap_cut(length, unit, count):
+    loads = np.full(count, (2.0**count - 0.5) / count)
+    loads[-1] -= 0.5
+    steps = np.array([[2.0 ** ((d - j) % count) for j in range(count)] for d in range(count)])
+    ends = np.rint(np.cumsum(np.linalg.solve(steps, loads)) * (length // unit)).astype(int) * unit
+    ends = [0] + [int(e) for e in ends]
+    return [(a, e - a) for a, e in zip(ends, ends[1:])]
+
+
+def gather_blocks(tok, blk, swaps, first, second, out, sems, halfway=None):
     send_sem, recv_sem, pass_send, pass_recv, swap_send, swap_recv, local_sem = sems
     t = lax.axis_index("tok")
     b = lax.axis_index("blk")
@@ -98,7 +108,7 @@
     count = len(dims)
     rows, cols = first.shape
     if swaps:
-        parts = [((o, n), (0, cols)) for o, n in cut(rows, 16, count)]
+        parts = [((o, n), (0, cols)) for o, n in (swap_cut if half > 1 else cut)(rows, 16, count)]
     else:
         parts = [((0, rows), (o, n)) for o, n in cut(cols, 128, count)]
 
@@ -233,14 +243,22 @@
         advance(0, p)
     begin(1)
     advance(0, count - 1)
-    for p in range(count):
-        advance(1, p)
-    for q in range(2):
+    for copy in locals_:
+        copy.wait()
+
+    def received(q):
         for j in range(count):
             for steps in range(2**count):
                 handed(q, j, steps, False).wait_recv()
-    for copy in locals_:
-        copy.wait()
+
+    if halfway is not None:
+        received(0)
+        halfway()
+    for p in range(count):
+        advance(1, p)
+    if halfway is None:
+        received(0)
+    received(1)
     for copy in pending:
         copy.wait_send()
 
@@ -284,7 +302,7 @@
 
 
 def newton_kernel(
-    tok, blk, tokens, first, second, gram, kept, came, g, square, left, inverse, sent,
+    tok, blk, tokens, rounded, gram, kept, came, g, square, left, inverse, sent,
     out_sem, in_sem, *sems
 ):
     width = g.shape[1]
@@ -292,18 +310,11 @@
     t = lax.axis_index("tok")
     b = lax.axis_index("blk")
     starts = row_starts(tok, blk, rows)
-    gather_blocks(tok, blk, False, first, second, g, sems)
     factor = 1.0 / (tokens * divisor)
     shift = damping / divisor
     eye = lax.broadcasted_iota(jnp.int32, (LANES, LANES), 0) == lax.broadcasted_iota(
         jnp.int32, (LANES, LANES), 1
     )
-
-    @pl.loop(0, width // LANES)
-    def _(i):
-        at = pl.ds(pl.multiple_of(i * LANES, LANES), LANES)
-        block = jnp.where(eye, g[at, at].astype(jnp.float32), 0.0)
-        inverse[:, at] = lax.rsqrt(jnp.sum(block, axis=0, keepdims=True) / tokens + epsilon)
 
     inverse_rows = []
     for s, start in enumerate(starts):
@@ -315,30 +326,54 @@
         inverse_rows += parts
     inverse_rows = jnp.concatenate(inverse_rows, axis=0)
 
-    def identity(i):
-        col = i * CHUNK + lax.broadcasted_iota(jnp.int32, (rows, CHUNK), 1)
-        row = lax.broadcasted_iota(jnp.int32, (rows, CHUNK), 0)
+    def identity(first_col, size):
+        col = first_col + lax.broadcasted_iota(jnp.int32, (rows, size), 1)
+        row = lax.broadcasted_iota(jnp.int32, (rows, size), 0)
         return jnp.concatenate(
             [(col - start == row).astype(jnp.float32) for start in starts], axis=0
         )
 
-    def scaled(i, at):
-        return gram[:, at] * factor * inverse_rows * inverse[:, at] + shift * identity(i)
+    def scaled(first_col, size):
+        at = pl.ds(first_col, size)
+        return gram[:, at] * factor * inverse_rows * inverse[:, at] + shift * identity(
+            first_col, size
+        )
+
+    half = blk // 2
+    depth = half * rows
+
+    def fold(side, add):
+        places = [pl.multiple_of((i * blk + side * half) * rows, LANES) for i in range(tok)]
+        for place in places:
+            for r in range(0, depth, LANES):
+                at = pl.ds(place + r, LANES)
+                block = jnp.where(eye, g[at, at].astype(jnp.float32), 0.0)
+                total = jnp.sum(block, axis=0, keepdims=True)
+                inverse[:, at] = lax.rsqrt(total / tokens + epsilon)
+            at = pl.ds(place, depth)
+            left[:, at] = (scaled(place, depth) * inverse[:, at]).astype(jnp.bfloat16)
+
+        @pl.loop(0, width // CHUNK)
+        def _(i):
+            at = pl.ds(pl.multiple_of(i * CHUNK, CHUNK), CHUNK)
+            total = square[:, at] if add else jnp.zeros((2 * rows, CHUNK), jnp.float32)
+            for place in places:
+                deep = pl.ds(place, depth)
+                total += jnp.dot(left[:, deep], g[deep, at], preferred_element_type=jnp.float32)
+            square[:, at] = total
+
+    side = b // half
+    gather_blocks(
+        tok, blk, False, rounded.at[pl.ds(0, rows)], rounded.at[pl.ds(rows, rows)], g, sems,
+        lambda: fold(side, False),
+    )
+    fold(1 - side, True)
 
     @pl.loop(0, width // CHUNK)
     def _(i):
-        at = pl.ds(pl.multiple_of(i * CHUNK, CHUNK), CHUNK)
-        left[:, at] = (scaled(i, at) * inverse[:, at]).astype(jnp.bfloat16)
-
-    @pl.loop(0, width // CHUNK)
-    def _(i):
-        at = pl.ds(pl.multiple_of(i * CHUNK, CHUNK), CHUNK)
-        product = jnp.dot(left[...], g[:, at], preferred_element_type=jnp.float32)
-        square[:, at] = product * (inverse[:, at] * factor) + shift * scaled(i, at)
-
-    @pl.loop(0, width // CHUNK)
-    def _(i):
-        at = pl.ds(pl.multiple_of(i * CHUNK, CHUNK), CHUNK)
+        start = pl.multiple_of(i * CHUNK, CHUNK)
+        at = pl.ds(start, CHUNK)
+        square[:, at] = square[:, at] * (inverse[:, at] * factor) + shift * scaled(start, CHUNK)
         left[:, at] = (square[:, at] * inverse[:, at]).astype(jnp.bfloat16)
 
     def swap(i):
@@ -359,7 +394,8 @@
         product = jnp.dot(left[...], g[:, at], preferred_element_type=jnp.float32)
         squared = square[:, at]
         cube = product * (inverse[:, at] * factor) + shift * squared
-        result = 4.0 * identity(i) - 6.0 * scaled(i, at) + 4.0 * squared - cube
+        start = pl.multiple_of(i * CHUNK, CHUNK)
+        result = 4.0 * identity(start, CHUNK) - 6.0 * scaled(start, CHUNK) + 4.0 * squared - cube
         kept[:, at] = result[:rows]
         sent[:, at] = result[rows:].astype(jnp.bfloat16)
 
@@ -426,7 +462,7 @@
             pltpu.SemaphoreType.DMA((steps,)),
             pltpu.SemaphoreType.DMA((steps,)),
         ],
-        tok, blk, 1, rounded[:rows], rounded[rows:], gram,
+        tok, blk, 1, rounded, gram,
     )
     came = came.astype(jnp.float32)
     return jnp.where(low, kept, came), jnp.where(low, came, kept)

time: 349 us -> 338 us (0.968)
  Pallas kernels: 338 us -> 330 us
    pallas_call x2, Pallas kernels: 338 us -> 330 us  [call(): pl.pallas_call(kernel, out_shape=outs, in_specs=[pl.BlockSpec(memory_spac...]
where the time goes in v3:
time: 338 us
  Pallas kernels  330 us (98%)
  other arithmetic  7.37 us (2%)
    pallas_call x2, Pallas kernels, call(): pl.pallas_call(kernel, out_shape=outs, in_specs=[pl.BlockSpec(memory_spac...  330 us

profile of v3, /device:TPU:0, one launch (start us, length us, event | category | flops | bytes accessed | tf_op | source)
XLA Modules:
  0.0 338.1 jit_solution(3943471684410277074)
XLA Ops:
  0.6 3.0 broadcast_select_fusion
  3.6 151.7 %shard_map.41 = (f32[256,4096]{1,0:T(8,128)}, bf16[256,4096]{1,0:T(8,128)(2,1)}) custom-call(bf16[512,1024]{1,0:T(8,128)(2,1)} %get-tuple-element.13.first, bf16[512,1024]{1,0:T(8,128)(2,1)} %get-tuple-element.12.second), custom_call_target="tpu_custom_call" | custom-call | tf_op jit(solution)/shard_map/pallas_call | solution.py:418
  155.3 178.4 %shard_map.42 = (f32[128,4096]{1,0:T(8,128)}, bf16[128,4096]{1,0:T(8,128)(2,1)}) custom-call(bf16[256,4096]{1,0:T(8,128)(2,1)} %get-tuple-element.6.rounded, f32[256,4096]{1,0:T(8,128)} %get-tuple-element.7.gram), custom_call_target="tpu_custom_call" | custom-call | tf_op jit(solution)/shard_map/pallas_call | solution.py:418
  333.7 4.4 %convert_select_fusion = (f32[128,4096]{1,0:T(8,128)}, f32[128,4096]{1,0:T(8,128)}) fusion(f32[128,4096]{1,0:T(8,128)} %get-tuple-element.8, bf16[128,4096]{1,0:T(8,128)(2,1)} %get-tuple-element.9, pred[]{:T(512)S(6)} %lt.3), kind=kLoop, calls=%fused_computation | loop fusion | flops 1572864 | bytes 7340033 | tf_op jit(solution)/shard_map/jit(_where)/select_n | solution.py:468
